TPU v7x, 128 devices: a whole 4x4x4 slice. The times are simulated.
128 devices in a mesh: gen: 16 (over x, z_hi, core), tp: 8 (over y, z_lo).
Axes of the slice: x: 4, y: 4, z: 4 (z_hi: 2, z_lo: 2; z = z_hi * 2 + z_lo), core: 2. Of those that a mesh axis runs over, the one named last changes fastest.
Arguments:
- hidden_in: bfloat16 [4, 32, 8192], P(None, 'gen'), may hold values from -6 to 6
- norm_gain: bfloat16 [8192], replicated, may hold values from 0.099609375 to 1.8984375
- w_query: bfloat16 [8192, 4096], P(('gen', 'tp')), may hold values from -0.0625 to 0.0625
- key_weight_matrix: bfloat16 [8192, 1024], P(('gen', 'tp')), may hold values from -0.0625 to 0.0625
- value_weight_matrix: bfloat16 [8192, 1024], P(('gen', 'tp')), may hold values from -0.0625 to 0.0625
- bias_query: bfloat16 [4096], P('tp'), may hold values from -3 to 3
- key_bias_vector: bfloat16 [1024], P('tp'), may hold values from -3 to 3
- value_bias_vector: bfloat16 [1024], P('tp'), may hold values from -3 to 3
- w_out: bfloat16 [4096, 8192], P(None, ('gen', 'tp')), may hold values from -0.09375 to 0.09375
- key_cache: bfloat16 [32, 8, 16384, 128], P('gen', 'tp'), may hold values from -400 to 400
- value_cache: bfloat16 [32, 8, 16384, 128], P('gen', 'tp'), may hold values from -16 to 16
- lengths: int32 [32], P('gen'), may hold values from 1 to 16384
- finished: int32 [32], P('gen'), may hold values 0 or 1
Outputs:
- layer_out: bfloat16 [4, 32, 8192], P(None, 'gen')
All inputs are finite; a program needn't handle non-finite values. No bound on the sum of `finished` on one device may be relied on, other than what follows from the above.
Results may differ from a plain program's by a relative error of at most 0.012.
Values may be sent and summed in bfloat16 or wider, within the bound.
A program may use at most 128 MiB of HBM per device.

v0:
```python
import math
import jax
import jax.numpy as jnp
from jax import lax
from jax.sharding import PartitionSpec as P

norm_eps = 1e-06
rope_base = 1000000.0
masked_score = -1e30


def sent_together(arrays, axis, dim, along):
    widths = [a.shape[along] for a in arrays]
    both = jnp.concatenate(arrays, axis=along)
    filled = lax.all_gather(both, axis, axis=dim, tiled=True)
    return tuple(jnp.split(filled, [sum(widths[:k]) for k in range(1, len(widths))], axis=along))


def from_everyone(array, axis):
    copies = jnp.broadcast_to(array, (lax.axis_size(axis), *array.shape))
    return lax.all_to_all(copies, axis, split_axis=0, concat_axis=0, tiled=True)


def of_everyone(array, axis):
    return from_everyone(array, axis).astype(jnp.float32).sum(axis=0)


def apply_rotation(values, token_positions):
    half_dim = values.shape[-1] // 2
    pair_index = jnp.arange(half_dim).astype(jnp.float32)
    frequency = jnp.exp(pair_index * (-2.0 * math.log(rope_base) / values.shape[-1]))
    angles = token_positions[..., None] * frequency
    lower_half = values[..., :half_dim]
    upper_half = values[..., half_dim:]
    cosine = jnp.cos(angles)
    sine = jnp.sin(angles)
    return jnp.concatenate(
        [lower_half * cosine - upper_half * sine, upper_half * cosine + lower_half * sine], axis=-1
    )


def attend(queries, new_key_rows, fresh_value_rows, key_cache, value_cache, live_length):
    step_count, row_count, query_heads, head_dim = queries.shape
    kv_heads = new_key_rows.shape[2]
    group_size = query_heads // kv_heads
    cache_len = key_cache.shape[2]
    block_len = min(cache_len, 2048)
    score_scale = 1.0 / math.sqrt(head_dim)
    grouped_heads = queries.reshape(step_count, row_count, kv_heads, group_size, head_dim)
    grouped_heads = jnp.transpose(grouped_heads, (1, 2, 3, 0, 4)).reshape(
        row_count, kv_heads, group_size * step_count, head_dim
    )
    fresh_keys = jnp.transpose(new_key_rows, (1, 2, 0, 3))
    fresh_values = jnp.transpose(fresh_value_rows, (1, 2, 0, 3))
    fresh_scores = (
        jnp.einsum("rkqd,rkud->rkqu", grouped_heads, fresh_keys, preferred_element_type=jnp.float32)
        * score_scale
    )
    query_step = jnp.arange(group_size * step_count) % step_count
    allowed = jnp.arange(step_count)[None, :] <= query_step[:, None]
    fresh_scores = jnp.where(allowed, fresh_scores, masked_score)
    running_max = jnp.max(fresh_scores, axis=-1)
    weights = jnp.exp(fresh_scores - running_max[..., None])
    running_sum = jnp.sum(weights, axis=-1)
    numerator = jnp.einsum(
        "rkqu,rkud->rkqd",
        weights.astype(jnp.bfloat16),
        fresh_values,
        preferred_element_type=jnp.float32,
    )
    block_count = (jnp.max(live_length) + block_len - 1) // block_len

    def visit(block_index, carry):
        running_max, running_sum, numerator = carry
        key_block = lax.dynamic_slice_in_dim(key_cache, block_index * block_len, block_len, 2)
        value_block = lax.dynamic_slice_in_dim(value_cache, block_index * block_len, block_len, 2)
        scores = (
            jnp.einsum(
                "rkqd,rkcd->rkqc", grouped_heads, key_block, preferred_element_type=jnp.float32
            )
            * score_scale
        )
        places = block_index * block_len + jnp.arange(block_len)
        inside = places[None, :] < live_length[:, None]
        scores = jnp.where(inside[:, None, None, :], scores, masked_score)
        new_max = jnp.maximum(running_max, jnp.max(scores, axis=-1))
        factor = jnp.exp(running_max - new_max)
        weights = jnp.exp(scores - new_max[..., None])
        running_sum = running_sum * factor + jnp.sum(weights, axis=-1)
        numerator = numerator * factor[..., None] + jnp.einsum(
            "rkqc,rkcd->rkqd",
            weights.astype(jnp.bfloat16),
            value_block,
            preferred_element_type=jnp.float32,
        )
        return (new_max, running_sum, numerator)

    running_max, running_sum, numerator = lax.fori_loop(
        0, block_count, visit, (running_max, running_sum, numerator)
    )
    result = numerator / running_sum[..., None]
    result = result.reshape(row_count, kv_heads, group_size, step_count, head_dim)
    result = jnp.transpose(result, (3, 0, 1, 2, 4)).reshape(
        step_count, row_count, query_heads * head_dim
    )
    return result.astype(jnp.bfloat16)


def shards(
    hidden_in,
    norm_gain,
    w_query,
    key_weight_matrix,
    value_weight_matrix,
    bias_query,
    key_bias_vector,
    value_bias_vector,
    w_out,
    key_cache,
    value_cache,
    lengths,
    finished,
):
    step_count, row_count, model_width = hidden_in.shape
    head_dim = key_cache.shape[3]
    kv_heads = key_cache.shape[1]
    query_heads = bias_query.shape[0] // head_dim
    widened = hidden_in.astype(jnp.float32)
    normed = (
        widened
        * lax.rsqrt(jnp.mean(widened * widened, axis=-1, keepdims=True) + norm_eps)
        * norm_gain.astype(jnp.float32)
    )
    normed = normed.astype(jnp.bfloat16)
    flattened = normed.reshape(step_count * row_count, model_width)
    query_part, key_part, value_part = (
        lax.all_to_all(w_query, "tp", split_axis=1, concat_axis=0, tiled=True),
        lax.all_to_all(key_weight_matrix, "tp", split_axis=1, concat_axis=0, tiled=True),
        lax.all_to_all(value_weight_matrix, "tp", split_axis=1, concat_axis=0, tiled=True),
    )
    out_part = lax.all_to_all(w_out, "tp", split_axis=0, concat_axis=1, tiled=True)
    segments = sent_together((query_part, key_part, value_part), "gen", 0, 1)
    first_sum = jnp.dot(flattened, segments[0], preferred_element_type=jnp.float32)
    second_sum = jnp.dot(flattened, segments[1], preferred_element_type=jnp.float32)
    third_sum = jnp.dot(flattened, segments[2], preferred_element_type=jnp.float32)
    queries = first_sum
    new_key_rows = second_sum
    fresh_value_rows = third_sum
    queries = queries + bias_query.astype(jnp.float32)
    new_key_rows = new_key_rows + key_bias_vector.astype(jnp.float32)
    fresh_value_rows = fresh_value_rows + value_bias_vector.astype(jnp.float32)
    token_positions = (lengths[None, :] + jnp.arange(step_count, dtype=jnp.int32)[:, None]).astype(
        jnp.float32
    )[:, :, None]
    rot_query = apply_rotation(
        queries.reshape(step_count, row_count, query_heads, head_dim), token_positions
    ).astype(jnp.bfloat16)
    rotated_key = apply_rotation(
        new_key_rows.reshape(step_count, row_count, kv_heads, head_dim), token_positions
    ).astype(jnp.bfloat16)
    value_rows_new = fresh_value_rows.reshape(step_count, row_count, kv_heads, head_dim).astype(
        jnp.bfloat16
    )
    live_length = jnp.where(finished != 0, 0, lengths)
    attended = attend(rot_query, rotated_key, value_rows_new, key_cache, value_cache, live_length)
    attended_flat = attended.reshape(step_count * row_count, query_heads * head_dim)
    partial_out = jnp.dot(
        attended_flat,
        lax.all_gather(out_part, "gen", axis=1, tiled=True),
        preferred_element_type=jnp.float32,
    )
    projected = of_everyone(partial_out.astype(jnp.bfloat16), "tp").astype(jnp.float32)
    projected = projected.reshape(step_count, row_count, model_width)
    layer_out = jnp.where(finished[None, :, None] != 0, widened, widened + projected)
    return layer_out.astype(jnp.bfloat16)


def solution(mesh):
    placed = (
        P(None, "gen", None),
        P(),
        P(("gen", "tp"), None),
        P(("gen", "tp"), None),
        P(("gen", "tp"), None),
        P("tp"),
        P("tp"),
        P("tp"),
        P(None, ("gen", "tp")),
        P("gen", "tp", None, None),
        P("gen", "tp", None, None),
        P("gen"),
        P("gen"),
    )
    return jax.shard_map(
        shards, mesh=mesh, in_specs=placed, out_specs=P(None, "gen", None), check_vma=False
    )
```

profile of v0, /device:TPU:0, one launch (start us, length us, event | category | flops | bytes accessed | tf_op | source)
XLA Modules:
  0.0 241.8 jit_solution(11346730564790892831)
XLA Ops:
  8.2 5.9 %all-to-all-start.1 = ((bf16[64,8,128]{2,0,1:T(8,128)(2,1)}), bf16[64,8,128]{2,0,1:T(8,128)(2,1)S(1)}, u32[]{:S(2)}, u32[]{:S(2)}) async-start(bf16[64,8,128]{2,0,1:T(8,128)(2,1)} %copy_bitcast_fusion.3), calls=%async_computation.1 | async-start | bytes 262144 | tf_op jit(solution)/shard_map/all_to_all | solution.py:138
  14.1 1.6 copy_bitcast_fusion.2
  15.7 4.8 %all-to-all-done.1 = bf16[64,8,128]{2,0,1:T(8,128)(2,1)S(1)} async-done(((bf16[64,8,128]{2,0,1:T(8,128)(2,1)}), bf16[64,8,128]{2,0,1:T(8,128)(2,1)S(1)}, u32[]{:S(2)}, u32[]{:S(2)}) %all-to-all-start.1) | async-done | bytes 131104 | tf_op jit(solution)/shard_map/all_to_all | solution.py:138
  20.5 3.4 %all-to-all-start.2 = ((bf16[64,8,128]{2,0,1:T(8,128)(2,1)}), bf16[64,8,128]{2,0,1:T(8,128)(2,1)S(1)}, u32[]{:S(2)}, u32[]{:S(2)}) async-start(bf16[64,8,128]{2,0,1:T(8,128)(2,1)} %copy_bitcast_fusion.2), calls=%async_computation.2 | async-start | bytes 262144 | tf_op jit(solution)/shard_map/all_to_all | solution.py:139
  24.0 1.1 copy.94
  25.1 5.2 %all-to-all-done.2 = bf16[64,8,128]{2,0,1:T(8,128)(2,1)S(1)} async-done(((bf16[64,8,128]{2,0,1:T(8,128)(2,1)}), bf16[64,8,128]{2,0,1:T(8,128)(2,1)S(1)}, u32[]{:S(2)}, u32[]{:S(2)}) %all-to-all-start.2) | async-done | bytes 131104 | tf_op jit(solution)/shard_map/all_to_all | solution.py:139
  30.3 11.0 %all_to_all.81 = bf16[64,8,512]{2,0,1:T(8,128)(2,1)S(1)} all-to-all(bf16[64,8,512]{2,0,1:T(8,128)(2,1)S(1)} %bitcast.117), channel_id=1, replica_groups=mesh['gen'=16,'tp'=8] {'tp'}, dimensions={1} | all-to-all | bytes 1048576 | tf_op jit(solution)/shard_map/all_to_all | solution.py:137
  41.3 1.0 pad_maximum_fusion
  42.3 1.1 copy.93
  43.4 11.4 %all_to_all.82 = bf16[8,512,64]{1,2,0:T(8,128)(2,1)} all-to-all(bf16[8,512,64]{1,2,0:T(8,128)(2,1)S(1)} %bitcast.118), channel_id=1, replica_groups=mesh['gen'=16,'tp'=8] {'tp'}, dimensions={0} | all-to-all | bytes 1048576 | tf_op jit(solution)/shard_map/all_to_all | solution.py:141
  54.8 1.3 fusion.59
  57.5 1.1 fusion.34
  59.4 73.8 %all-gather.3.cloned.1.call-done = bf16[8192,768]{1,0:T(8,128)(2,1)} async-done(((bf16[512,768]{1,0:T(8,128)(2,1)}), bf16[8192,768]{1,0:T(8,128)(2,1)}) %all-gather.3.cloned.1.call-update) | async-done | bytes 12582928 | tf_op jit(solution)/shard_map/all_gather | solution.py:15
  133.2 4.7 %fusion.21 = f32[8,512]{1,0:T(8,128)S(1)} fusion(bf16[8,8192]{1,0:T(8,128)(2,1)S(1)} %reshape.254, bf16[8192,768]{1,0:T(8,128)(2,1)} %all-gather.3.cloned.1.call-done, f32[512]{0:T(512)S(1)} %convert_element_type.99), kind=kOutput, calls=%fused_computation.31 | convolution fusion | flops 67112960 | bytes 8538112 | tf_op jit(solution)/shard_map/dot_general | solution.py:143
  138.1 2.0 fusion.24
  140.5 2.0 fusion.31
  142.6 18.1 %while.14 = (s32[]{:T(128)}, f32[2,1,16]{2,0,1:T(2,128)S(1)}, f32[2,1,16]{2,0,1:T(2,128)S(1)}, f32[2,1,16,128]{3,2,0,1:T(8,128)S(1)}, s32[]{:T(128)}, /*index=5*...) while((s32[]{:T(128)}, f32[2,1,16]{2,0,1:T(2,128)S(1)}, ...), condition=%wide.region_7.8_spmd, body=%wide.region_4.7_spmd.sunk | while | flops 34027620 | bytes 2951359 | solution.py:98
  142.7 1.8 fusion.78
  144.5 1.5 fusion.81
  146.4 1.7 fusion.78
  148.1 1.5 fusion.81
  150.0 1.7 fusion.78
  151.8 1.5 fusion.81
  153.7 1.7 fusion.78
  155.4 1.6 fusion.81
  157.3 1.7 fusion.78
  159.0 1.6 fusion.81
  160.9 45.1 %all-gather.5.cloned.1.call-done = bf16[512,8192]{0,1:T(8,128)(2,1)} async-done(((bf16[512,512]{0,1:T(8,128)(2,1)}), bf16[512,8192]{0,1:T(8,128)(2,1)}) %all-gather.5.cloned.1.call-update) | async-done | bytes 8388624 | tf_op jit(solution)/shard_map/all_gather | solution.py:169
  206.0 5.6 %convolution_convert_fusion = bf16[8,8192]{1,0:T(8,128)(2,1)S(1)} fusion(bf16[512,8192]{0,1:T(8,128)(2,1)} %all-gather.5.cloned.1.call-done, bf16[1,8,4,128]{3,2,1,0:T(4,128)(2,1)S(1)} %bitcast.128), kind=kOutput, calls=%fused_computation.22 | convolution fusion | flops 67174400 | bytes 8527872 | tf_op jit(solution)/shard_map/dot_general | solution.py:167
  211.6 1.1 broadcast_in_dim.37
  212.7 4.4 %all-to-all-start.4 = ((bf16[8,8,8192]{2,1,0:T(8,128)(2,1)}), bf16[8,8,8192]{2,1,0:T(8,128)(2,1)S(1)}, u32[]{:S(2)}, u32[]{:S(2)}) async-start(bf16[8,8,8192]{2,1,0:T(8,128)(2,1)} %broadcast_in_dim.37), calls=%async_computation.4 | async-start | bytes 2097152 | tf_op jit(solution)/shard_map/all_to_all | solution.py:21
  217.0 16.7 %all-to-all-done.4 = bf16[8,8,8192]{2,1,0:T(8,128)(2,1)S(1)} async-done(((bf16[8,8,8192]{2,1,0:T(8,128)(2,1)}), bf16[8,8,8192]{2,1,0:T(8,128)(2,1)S(1)}, u32[]{:S(2)}, u32[]{:S(2)}) %all-to-all-start.4) | async-done | bytes 1048608 | tf_op jit(solution)/shard_map/all_to_all | solution.py:21
  (77 shorter events, 6.8 us)
Async XLA Ops:
  6.5 1.0 copy-start
  6.5 52.5 %copy-start.3 = (s32[2]{0:T(128)S(1)}, s32[2]{0:T(128)}, u32[]{:S(2)}) copy-start(s32[2]{0:T(128)} %param.26) | copy-start | bytes 28
  6.5 52.2 %copy-start.1 = (bf16[4,2,8192]{2,1,0:T(2,128)(2,1)S(1)}, bf16[4,2,8192]{2,1,0:T(2,128)(2,1)}, u32[]{:S(2)}) copy-start(bf16[4,2,8192]{2,1,0:T(2,128)(2,1)} %param.15) | copy-start | bytes 393220
  6.5 52.4 %copy-start.2 = (bf16[512]{0:T(512)(128)(2,1)S(1)}, bf16[512]{0:T(512)(128)(2,1)}, u32[]{:S(2)}) copy-start(bf16[512]{0:T(512)(128)(2,1)} %param.20) | copy-start | bytes 3076
  6.5 52.6 %copy-start.5 = (bf16[128]{0:T(256)(128)(2,1)S(1)}, bf16[128]{0:T(256)(128)(2,1)}, u32[]{:S(2)}) copy-start(bf16[128]{0:T(256)(128)(2,1)} %param.21) | copy-start | bytes 772
  6.5 52.6 %copy-start.6 = (bf16[128]{0:T(256)(128)(2,1)S(1)}, bf16[128]{0:T(256)(128)(2,1)}, u32[]{:S(2)}) copy-start(bf16[128]{0:T(256)(128)(2,1)} %param.22) | copy-start | bytes 772
  8.2 12.3 %all-to-all-start.1 = ((bf16[64,8,128]{2,0,1:T(8,128)(2,1)}), bf16[64,8,128]{2,0,1:T(8,128)(2,1)S(1)}, u32[]{:S(2)}, u32[]{:S(2)}) async-start(bf16[64,8,128]{2,0,1:T(8,128)(2,1)} %copy_bitcast_fusion.3), calls=%async_computation.1 | async-start | bytes 262144 | tf_op jit(solution)/shard_map/all_to_all | solution.py:138
  20.5 9.7 %all-to-all-start.2 = ((bf16[64,8,128]{2,0,1:T(8,128)(2,1)}), bf16[64,8,128]{2,0,1:T(8,128)(2,1)S(1)}, u32[]{:S(2)}, u32[]{:S(2)}) async-start(bf16[64,8,128]{2,0,1:T(8,128)(2,1)} %copy_bitcast_fusion.2), calls=%async_computation.2 | async-start | bytes 262144 | tf_op jit(solution)/shard_map/all_to_all | solution.py:139
  23.9 109.2 %all-gather.3.cloned.1.call-start = ((), (), s32[]{:S(2)}) async-start(), calls=%async_computation.5 | async-start | bytes 13369344 | tf_op jit(solution)/shard_map/all_gather | solution.py:15
  42.3 163.7 %all-gather.5.cloned.1.call-start = ((), (), s32[]{:S(2)}) async-start(), calls=%async_computation.6 | async-start | bytes 8912896 | tf_op jit(solution)/shard_map/all_gather | solution.py:169
  160.8 56.3 %copy-start.4 = (s32[2]{0:T(128)S(1)}, s32[2]{0:T(128)}, u32[]{:S(2)}) copy-start(s32[2]{0:T(128)} %param.27) | copy-start | bytes 28
  212.7 21.1 %all-to-all-start.4 = ((bf16[8,8,8192]{2,1,0:T(8,128)(2,1)}), bf16[8,8,8192]{2,1,0:T(8,128)(2,1)S(1)}, u32[]{:S(2)}, u32[]{:S(2)}) async-start(bf16[8,8,8192]{2,1,0:T(8,128)(2,1)} %broadcast_in_dim.37), calls=%async_computation.4 | async-start | bytes 2097152 | tf_op jit(solution)/shard_map/all_to_all | solution.py:21
Sparse Core Ops, SparseCore 0:
  42.4 90.7 all-gather.2
  135.6 70.3 all-gather.4
where the time goes:
time: 243 us; the launch traced here: 242 us
  waiting for transfers between devices  146 us (60%)
  matrix products  31 us (13%)
  blocking collectives  22.4 us (9%)
  between operations  14.3 us (6%)
  starting transfers between devices  13.8 us (6%)
  other arithmetic  7.55 us (3%)
  local copies, waits for them, and re-layouts  6.9 us (3%)
    all_gather x1, waiting for transfers between devices, sent_together(): filled = lax.all_gather(both, axis, axis=dim, tiled=True)  73.8 us
    all_gather x1, waiting for transfers between devices, shards(): lax.all_gather(out_part, 'gen', axis=1, tiled=True)  45.1 us
    all_to_all x1, waiting for transfers between devices, from_everyone(): return lax.all_to_all(copies, axis, split_axis=0, concat_axis=0, tiled=True)  16.7 us
    all_to_all x1, blocking collectives, shards(): lax.all_to_all(w_out, 'tp', split_axis=0, concat_axis=1, tiled=True)  11.4 us
    all_to_all x1, blocking collectives, shards(): lax.all_to_all(w_query, 'tp', split_axis=1, concat_axis=0, tiled=True)  11 us
    dot_general x5, matrix products, visit(): jnp.einsum('rkqd,rkcd->rkqc', grouped_heads, key_block, preferred_element...  8.59 us
    dot_general x5, matrix products, visit(): jnp.einsum('rkqc,rkcd->rkqd', weights.astype(jnp.bfloat16), value_block,...  7.75 us
    all_to_all x1, starting transfers between devices, shards(): lax.all_to_all(key_weight_matrix, 'tp', split_axis=1, concat_axis=0, tile...  5.94 us
  transfers between devices with their start and end apart: 5, of which 5 were waited for; matrix products, arithmetic and copies ran while one was open for 14% of the time, Pallas kernels for 0%

commit v1 on v0

--- a/solution.py
+++ b/solution.py
@@ -7,6 +7,11 @@
 norm_eps = 1e-06
 rope_base = 1000000.0
 masked_score = -1e30
+
+
+def all_by_exchange(block, name, dim):
+    stack = jnp.stack([block] * lax.axis_size(name))
+    return jnp.concatenate(lax.all_to_all(stack, name, 0, 0), axis=dim)
 
 
 def sent_together(arrays, axis, dim, along):
@@ -165,9 +170,7 @@
     attended = attend(rot_query, rotated_key, value_rows_new, key_cache, value_cache, live_length)
     attended_flat = attended.reshape(step_count * row_count, query_heads * head_dim)
     partial_out = jnp.dot(
-        attended_flat,
-        lax.all_gather(out_part, "gen", axis=1, tiled=True),
-        preferred_element_type=jnp.float32,
+        attended_flat, all_by_exchange(out_part, "gen", 1), preferred_element_type=jnp.float32
     )
     projected = of_everyone(partial_out.astype(jnp.bfloat16), "tp").astype(jnp.float32)
     projected = projected.reshape(step_count, row_count, model_width)

time: 243 us -> 292 us (1.20)
  the two profiles are of different devices: /device:TPU:0 before, /device:TPU:4 now
where the time goes in v1:
time: 292 us; the launch traced here: 291 us
  waiting for transfers between devices  182 us (62%)
  matrix products  37.4 us (13%)
  starting transfers between devices  24.2 us (8%)
  between operations  14.3 us (5%)
  local copies, waits for them, and re-layouts  11.7 us (4%)
  blocking collectives  11 us (4%)
  other arithmetic  9.79 us (3%)
    all_gather x1, waiting for transfers between devices, sent_together(): filled = lax.all_gather(both, axis, axis=dim, tiled=True)  153 us
    all_to_all x1, waiting for transfers between devices, from_everyone(): return lax.all_to_all(copies, axis, split_axis=0, concat_axis=0, tiled=True)  17.3 us
    dot_general x7, matrix products, visit(): jnp.einsum('rkqd,rkcd->rkqc', grouped_heads, key_block, preferred_element...  11.9 us
    all_to_all x1, blocking collectives, shards(): lax.all_to_all(w_query, 'tp', split_axis=1, concat_axis=0, tiled=True)  11 us
    dot_general x7, matrix products, visit(): jnp.einsum('rkqc,rkcd->rkqd', weights.astype(jnp.bfloat16), value_block,...  10.8 us
    all_to_all x1, starting transfers between devices, all_by_exchange(): return jnp.concatenate(lax.all_to_all(stack, name, 0, 0), axis=dim)  7.91 us
  transfers between devices with their start and end apart: 6, of which 5 were waited for; matrix products, arithmetic and copies ran while one was open for 17% of the time, Pallas kernels for 0%

profile of v1, /device:TPU:4, one launch (start us, length us, event | category | flops | bytes accessed | tf_op | source)
XLA Modules:
  0.0 290.8 jit_solution(6526511319194498407)
XLA Ops:
  8.1 5.8 %all-to-all-start.1 = ((bf16[64,8,128]{2,0,1:T(8,128)(2,1)}), bf16[64,8,128]{2,0,1:T(8,128)(2,1)S(1)}, u32[]{:S(2)}, u32[]{:S(2)}) async-start(bf16[64,8,128]{2,0,1:T(8,128)(2,1)} %copy_bitcast_fusion.3), calls=%async_computation.1 | async-start | bytes 262144 | tf_op jit(solution)/shard_map/all_to_all | solution.py:143
  13.9 1.6 copy_bitcast_fusion.2
  15.5 4.8 %all-to-all-done.1 = bf16[64,8,128]{2,0,1:T(8,128)(2,1)S(1)} async-done(((bf16[64,8,128]{2,0,1:T(8,128)(2,1)}), bf16[64,8,128]{2,0,1:T(8,128)(2,1)S(1)}, u32[]{:S(2)}, u32[]{:S(2)}) %all-to-all-start.1) | async-done | bytes 131104 | tf_op jit(solution)/shard_map/all_to_all | solution.py:143
  20.3 3.4 %all-to-all-start.2 = ((bf16[64,8,128]{2,0,1:T(8,128)(2,1)}), bf16[64,8,128]{2,0,1:T(8,128)(2,1)S(1)}, u32[]{:S(2)}, u32[]{:S(2)}) async-start(bf16[64,8,128]{2,0,1:T(8,128)(2,1)} %copy_bitcast_fusion.2), calls=%async_computation.2 | async-start | bytes 262144 | tf_op jit(solution)/shard_map/all_to_all | solution.py:144
  24.9 5.2 %all-to-all-done.2 = bf16[64,8,128]{2,0,1:T(8,128)(2,1)S(1)} async-done(((bf16[64,8,128]{2,0,1:T(8,128)(2,1)}), bf16[64,8,128]{2,0,1:T(8,128)(2,1)S(1)}, u32[]{:S(2)}, u32[]{:S(2)}) %all-to-all-start.2) | async-done | bytes 131104 | tf_op jit(solution)/shard_map/all_to_all | solution.py:144
  30.1 11.0 %all_to_all.83 = bf16[64,8,512]{2,0,1:T(8,128)(2,1)S(1)} all-to-all(bf16[64,8,512]{2,0,1:T(8,128)(2,1)S(1)} %bitcast.120), channel_id=1, replica_groups=mesh['gen'=16,'tp'=8] {'tp'}, dimensions={1} | all-to-all | bytes 1048576 | tf_op jit(solution)/shard_map/all_to_all | solution.py:142
  42.1 1.9 copy.93
  44.0 3.5 %all-to-all-start.3 = ((bf16[8,512,64]{1,2,0:T(8,128)(2,1)}), bf16[8,512,64]{1,2,0:T(8,128)(2,1)S(1)}, u32[]{:S(2)}, u32[]{:S(2)}) async-start(bf16[8,512,64]{1,2,0:T(8,128)(2,1)} %bitcast.100), calls=%async_computation.3 | async-start | bytes 1048576 | tf_op jit(solution)/shard_map/all_to_all | solution.py:146
  53.6 2.0 all-to-all-done.3
  55.6 4.1 %stack.5 = bf16[16,512,512]{1,2,0:T(8,128)(2,1)} broadcast(bf16[512,512]{0,1:T(8,128)(2,1)S(1)} %bitcast.118), dimensions={1,2} | broadcast | bytes 8912896 | tf_op jit(solution)/shard_map/stack | solution.py:13
  59.7 7.9 %all-to-all-start.4 = ((bf16[16,512,512]{1,2,0:T(8,128)(2,1)}), bf16[16,512,512]{1,2,0:T(8,128)(2,1)}, u32[]{:S(2)}, u32[]{:S(2)}) async-start(bf16[16,512,512]{1,2,0:T(8,128)(2,1)} %stack.5), calls=%async_computation.4 | async-start | bytes 16777216 | tf_op jit(solution)/shard_map/all_to_all | solution.py:14
  67.6 152.8 %all-gather.2.cloned.1.call-done = bf16[8192,768]{1,0:T(8,128)(2,1)} async-done(((bf16[512,768]{1,0:T(8,128)(2,1)}), bf16[8192,768]{1,0:T(8,128)(2,1)}) %all-gather.2.cloned.1.call-update) | async-done | bytes 12582928 | tf_op jit(solution)/shard_map/all_gather | solution.py:20
  220.4 4.7 %fusion.21 = f32[8,512]{1,0:T(8,128)S(1)} fusion(bf16[8,8192]{1,0:T(8,128)(2,1)S(1)} %reshape.263, bf16[8192,768]{1,0:T(8,128)(2,1)} %all-gather.2.cloned.1.call-done, f32[512]{0:T(512)S(1)} %convert_element_type.99), kind=kOutput, calls=%fused_computation.31 | convolution fusion | flops 67112960 | bytes 8538112 | tf_op jit(solution)/shard_map/dot_general | solution.py:148
  225.2 2.0 fusion.24
  227.7 2.0 fusion.31
  229.8 25.2 %while.14 = (s32[]{:T(128)}, f32[2,1,16]{2,0,1:T(2,128)S(1)}, f32[2,1,16]{2,0,1:T(2,128)S(1)}, f32[2,1,16,128]{3,2,0,1:T(8,128)S(1)}, s32[]{:T(128)}, /*index=5*...) while((s32[]{:T(128)}, f32[2,1,16]{2,0,1:T(2,128)S(1)}, ...), condition=%wide.region_7.8_spmd, body=%wide.region_4.7_spmd.sunk | while | flops 34027620 | bytes 2951359 | solution.py:103
  229.9 1.7 fusion.78
  231.7 1.5 fusion.81
  233.6 1.7 fusion.78
  235.3 1.5 fusion.81
  237.2 1.7 fusion.78
  238.9 1.5 fusion.81
  240.8 1.7 fusion.78
  242.5 1.5 fusion.81
  244.4 1.7 fusion.78
  246.1 1.5 fusion.81
  248.0 1.7 fusion.78
  249.7 1.5 fusion.81
  251.6 1.7 fusion.78
  255.2 5.7 %convolution_convert_fusion = bf16[8,8192]{1,0:T(8,128)(2,1)S(1)} fusion(bf16[512,8192]{0,1:T(8,128)(2,1)} %bitcast.37, bf16[1,8,4,128]{3,2,1,0:T(4,128)(2,1)S(1)} %bitcast.130), kind=kOutput, calls=%fused_computation.22 | convolution fusion | flops 67174400 | bytes 8527872 | tf_op jit(solution)/shard_map/dot_general | solution.py:172
  261.9 3.6 %all-to-all-start.5 = ((bf16[8,8,8192]{2,1,0:T(8,128)(2,1)}), bf16[8,8,8192]{2,1,0:T(8,128)(2,1)S(1)}, u32[]{:S(2)}, u32[]{:S(2)}) async-start(bf16[8,8,8192]{2,1,0:T(8,128)(2,1)} %broadcast_in_dim.37), calls=%async_computation.5 | async-start | bytes 2097152 | tf_op jit(solution)/shard_map/all_to_all | solution.py:26
  265.5 17.3 %all-to-all-done.5 = bf16[8,8,8192]{2,1,0:T(8,128)(2,1)S(1)} async-done(((bf16[8,8,8192]{2,1,0:T(8,128)(2,1)}), bf16[8,8,8192]{2,1,0:T(8,128)(2,1)S(1)}, u32[]{:S(2)}, u32[]{:S(2)}) %all-to-all-start.5) | async-done | bytes 1048608 | tf_op jit(solution)/shard_map/all_to_all | solution.py:26
  (92 shorter events, 16.0 us)
Async XLA Ops:
  6.5 0.9 copy-start
  6.5 46.8 %copy-start.2 = (bf16[512]{0:T(512)(128)(2,1)S(1)}, bf16[512]{0:T(512)(128)(2,1)}, u32[]{:S(2)}) copy-start(bf16[512]{0:T(512)(128)(2,1)} %param.20) | copy-start | bytes 3076
  6.5 46.9 %copy-start.4 = (bf16[128]{0:T(256)(128)(2,1)S(1)}, bf16[128]{0:T(256)(128)(2,1)}, u32[]{:S(2)}) copy-start(bf16[128]{0:T(256)(128)(2,1)} %param.21) | copy-start | bytes 772
  6.5 46.9 %copy-start.5 = (bf16[128]{0:T(256)(128)(2,1)S(1)}, bf16[128]{0:T(256)(128)(2,1)}, u32[]{:S(2)}) copy-start(bf16[128]{0:T(256)(128)(2,1)} %param.22) | copy-start | bytes 772
  8.1 12.2 %all-to-all-start.1 = ((bf16[64,8,128]{2,0,1:T(8,128)(2,1)}), bf16[64,8,128]{2,0,1:T(8,128)(2,1)S(1)}, u32[]{:S(2)}, u32[]{:S(2)}) async-start(bf16[64,8,128]{2,0,1:T(8,128)(2,1)} %copy_bitcast_fusion.3), calls=%async_computation.1 | async-start | bytes 262144 | tf_op jit(solution)/shard_map/all_to_all | solution.py:143
  20.3 9.7 %all-to-all-start.2 = ((bf16[64,8,128]{2,0,1:T(8,128)(2,1)}), bf16[64,8,128]{2,0,1:T(8,128)(2,1)S(1)}, u32[]{:S(2)}, u32[]{:S(2)}) async-start(bf16[64,8,128]{2,0,1:T(8,128)(2,1)} %copy_bitcast_fusion.2), calls=%async_computation.2 | async-start | bytes 262144 | tf_op jit(solution)/shard_map/all_to_all | solution.py:144
  23.7 196.6 %all-gather.2.cloned.1.call-start = ((), (), s32[]{:S(2)}) async-start(), calls=%async_computation.6 | async-start | bytes 13369344 | tf_op jit(solution)/shard_map/all_gather | solution.py:20
  44.0 11.6 %all-to-all-start.3 = ((bf16[8,512,64]{1,2,0:T(8,128)(2,1)}), bf16[8,512,64]{1,2,0:T(8,128)(2,1)S(1)}, u32[]{:S(2)}, u32[]{:S(2)}) async-start(bf16[8,512,64]{1,2,0:T(8,128)(2,1)} %bitcast.100), calls=%async_computation.3 | async-start | bytes 1048576 | tf_op jit(solution)/shard_map/all_to_all | solution.py:146
  59.7 195.5 %all-to-all-start.4 = ((bf16[16,512,512]{1,2,0:T(8,128)(2,1)}), bf16[16,512,512]{1,2,0:T(8,128)(2,1)}, u32[]{:S(2)}, u32[]{:S(2)}) async-start(bf16[16,512,512]{1,2,0:T(8,128)(2,1)} %stack.5), calls=%async_computation.4 | async-start | bytes 16777216 | tf_op jit(solution)/shard_map/all_to_all | solution.py:14
  255.1 10.4 %copy-start.3 = (s32[2]{0:T(128)S(1)}, s32[2]{0:T(128)}, u32[]{:S(2)}) copy-start(s32[2]{0:T(128)} %param.27) | copy-start | bytes 28
  255.2 27.9 %copy-start.1 = (bf16[4,2,8192]{2,1,0:T(2,128)(2,1)S(1)}, bf16[4,2,8192]{2,1,0:T(2,128)(2,1)}, u32[]{:S(2)}) copy-start(bf16[4,2,8192]{2,1,0:T(2,128)(2,1)} %param.15) | copy-start | bytes 393220
  261.9 20.9 %all-to-all-start.5 = ((bf16[8,8,8192]{2,1,0:T(8,128)(2,1)}), bf16[8,8,8192]{2,1,0:T(8,128)(2,1)S(1)}, u32[]{:S(2)}, u32[]{:S(2)}) async-start(bf16[8,8,8192]{2,1,0:T(8,128)(2,1)} %broadcast_in_dim.37), calls=%async_computation.5 | async-start | bytes 2097152 | tf_op jit(solution)/shard_map/all_to_all | solution.py:26
Sparse Core Ops, SparseCore 0:
  42.2 178.0 all-gather.1
